TPU v7x, 128 devices: a whole 4x4x4 slice. The times are simulated.
128 devices in a mesh: layer: 4 (over x_lo, core), feat: 32 (over x_hi, y, z).
Axes of the slice: x: 4 (x_hi: 2, x_lo: 2; x = x_hi * 2 + x_lo), y: 4, z: 4, core: 2. Of those that a mesh axis runs over, the one named last changes fastest.
Arguments:
- inputs: bfloat16 [4, 512, 2304], P('layer', 'feat'), may hold values from -6 to 6
- targets: bfloat16 [4, 512, 2304], P('layer', 'feat'), may hold values from -64 to 64
- enc_weight: bfloat16 [4, 2304, 8192], P('layer', None, 'feat'), may hold values from -0.125 to 0.125
- enc_bias: float32 [4, 8192], P('layer', 'feat'), may hold values from -3 to 3
- dec_weight: bfloat16 [4, 4, 8192, 2304], P('layer', None, 'feat'), may hold values from -0.0625 to 0.0625
- dec_bias: float32 [4, 2304], P('layer'), may hold values from -3 to 3
Outputs:
- enc_grad: float32 [4, 2304, 8192], P('layer', None, 'feat')
- enc_bias_grad: float32 [4, 8192], P('layer', 'feat')
- dec_grad: float32 [4, 4, 8192, 2304], P('layer', None, 'feat')
- dec_bias_grad: float32 [4, 2304], P('layer')
- mean_square: float32 [], replicated
All inputs are finite; a program needn't handle non-finite values.
Results may differ from a plain program's by a relative error of at most 0.0095.
Values may be sent and summed in bfloat16 or wider, within the bound.
No kernel may reach another device: no remote copies, remote signals or barrier semaphores. Data moves between devices by JAX's collectives and lax.ppermute only.
A program may use at most 128 MiB of HBM per device.

v0:
```python
import jax
import jax.numpy as jnp
from jax import lax
from jax.experimental.layout import Layout, with_layout_constraint
from jax.sharding import Mesh, PartitionSpec as P


MB = 128
ROW_MAJOR = Layout(major_to_minor=(0, 1, 2))
AXES = ("x_lo", "core", "x_hi", "y", "z")
SIZES = (2, 2, 2, 4, 4)
LAYER = ("x_lo", "core")
FEAT = ("x_hi", "y", "z")
bf16, f32 = jnp.bfloat16, jnp.float32


PLANE = ("core", "y", "z")


def route(ring, step):
    pairs = []
    for device in range(32):
        core, y, z = device // 16, device // 4 % 4, device % 4
        if (ring == "u") == (core == 0):
            to = core * 16 + (y + step) % 4 * 4 + z
        else:
            to = core * 16 + y * 4 + (z + step) % 4
        pairs.append((device, to))
    return pairs


def move(value, ring, step):
    return lax.ppermute(value, PLANE, route(ring, step))


def swap(value, axis):
    return lax.ppermute(value, axis, [(0, 1), (1, 0)])


def gather4(value, ring):
    far, up, down = move(value, ring, 2), move(value, ring, -1), move(value, ring, 1)
    return [value, up, far, down]


def scatter4(blocks, ring):
    arrived = []
    for k in (2, 1, 3):
        arrived.append(move(blocks[k], ring, k))
    total = blocks[0].astype(f32)
    for piece in arrived:
        total = total + piece.astype(f32)
    return total


def relay4(value, ring):
    up, down = move(value, ring, -1), move(value, ring, 1)
    half = value.shape[0] // 2
    far = jnp.concatenate([move(up[:half], ring, -1), move(down[half:], ring, 1)])
    return [value, up, far, down]


ACROSS = [(0, 3), (1, 2), (2, 1), (3, 0)]


def turned(value):
    shape = value.shape
    return value.reshape(4, 4, shape[0] // 16, *shape[1:]).swapaxes(0, 1).reshape(shape)


def body(inputs, targets, enc_weight, enc_bias, dec_weight, dec_bias):
    x_lo = lax.axis_index("x_lo")
    core = lax.axis_index("core")
    layer = 2 * x_lo + core
    features = enc_weight.shape[2]
    rows, width = inputs.shape[1:]
    tokens = 32 * rows

    both = jnp.concatenate([inputs[0], swap(inputs[0], "x_hi")])
    column = jnp.concatenate(gather4(both, "v"))
    both, dec_weight = lax.optimization_barrier((both, dec_weight))
    tokens_in = jnp.concatenate(relay4(column, "u"))

    pairs = dec_weight[0].reshape(2, 2, features, width)
    keep = lax.dynamic_index_in_dim(pairs, core, 1, keepdims=False)
    give = lax.dynamic_index_in_dim(pairs, 1 - core, 1, keepdims=False)
    got = swap(give, "core")
    slot = 2 * jnp.arange(2, dtype=jnp.int32)
    own_valid = (slot + core >= layer).astype(bf16)[:, None, None]
    pair_valid = (slot + core >= layer + 1 - 2 * core).astype(bf16)[:, None, None]
    weight = jnp.concatenate([keep * own_valid, got * pair_valid], axis=1)

    pre_act = jnp.dot(tokens_in, enc_weight[0], preferred_element_type=f32) + enc_bias[0]
    activity = jnp.maximum(pre_act, 0.0).astype(bf16)
    act_pair = jnp.concatenate([activity, turned(swap(activity, "core"))], axis=1)

    blocks = act_pair.reshape(4, tokens // 4, 2 * features)
    partial = [None] * 4
    for k in (2, 1, 3, 0):
        partial[k] = jnp.einsum(
            "tf,sfd->std", blocks[k], weight, preferred_element_type=f32
        ).astype(bf16)

    partial[0] = lax.optimization_barrier(with_layout_constraint(partial[0], ROW_MAJOR))
    total = scatter4(partial, "u").astype(bf16).reshape(2, 4, 2 * rows, width)
    total = scatter4([total[:, k] for k in range(4)], "v").reshape(2, 2, rows, width)

    shift = dec_bias[0] - targets[0].astype(f32)
    owner = (jnp.arange(2) == x_lo).astype(f32)[:, None, None]
    total = jnp.stack([total[:, 0] + owner * shift, total[:, 1]], axis=1)
    terms = total.astype(bf16)
    partner = swap(terms, "x_hi")
    same = swap(terms[1], "x_lo")
    other = lax.ppermute(terms[1], ("x_lo", "x_hi"), ACROSS)
    residual = terms.astype(f32) + partner[:, ::-1].astype(f32)
    second = residual[1] + same.astype(f32) + other[::-1].astype(f32)
    error = jnp.stack([residual[0], second]).astype(bf16).reshape(2, 2 * rows, width)
    column = jnp.concatenate(
        [piece[:, None] for piece in gather4(error, "v")], axis=1
    )
    mine = relay4(column.reshape(2, tokens // 4, width), "u")
    pair = [swap(piece, "core") for piece in mine]

    def back(piece, slot):
        return lax.dot_general(
            piece[slot], weight[slot], (((1,), (1,)), ((), ())), preferred_element_type=f32
        )

    grad_both = jnp.concatenate([back(piece, 0) + back(piece, 1) for piece in mine])
    grad_act = (grad_both[:, :features] + turned(swap(grad_both[:, features:], "core"))) / MB
    grad_pre = jnp.where(pre_act > 0, grad_act, 0.0)
    enc_bias_grad = jnp.sum(grad_pre, axis=0)[None]
    enc_grad = lax.dot_general(
        tokens_in,
        grad_pre.astype(bf16),
        (((0,), (0,)), ((), ())),
        preferred_element_type=f32,
    )[None]

    errors = [[jnp.concatenate([p[k] for p in held]) for k in range(2)] for held in (mine, pair)]
    orders = (activity, turned(activity))
    slots = []
    for target in range(4):
        parity = core == target % 2
        err = jnp.where(parity, errors[0][target // 2], errors[1][target // 2])
        act = jnp.where(parity, *orders)
        grad = lax.dot_general(act, err, (((0,), (0,)), ((), ())), preferred_element_type=f32)
        slots.append(jnp.where(target >= layer, grad / MB, 0.0))
    dec_grad = jnp.stack(slots)

    ones = jnp.ones((8, tokens // 4), bf16)
    same_row = jnp.eye(tokens // 4, dtype=f32)
    sums, grams = 0.0, 0.0
    for piece in mine:
        sums = sums + jnp.einsum("rt,std->srd", ones, piece, preferred_element_type=f32)
        grams = grams + jnp.einsum("std,sud->stu", piece, piece, preferred_element_type=f32)
    sums = lax.dynamic_index_in_dim(sums, x_lo, 0, keepdims=False)[0]
    squares = jnp.sum(grams * same_row)
    dec_bias_grad = (sums / MB)[None]
    square = jnp.broadcast_to(squares, (8, 128))
    square = square + swap(square, "core")
    square = jnp.where(x_lo == 0, square, lax.ppermute(square, "x_lo", [(0, 1)]))
    mean_square = square[0, 0] / (4 * tokens * width)
    return (enc_grad, enc_bias_grad, dec_grad[None], dec_bias_grad, mean_square)


def solution(mesh):
    fine = Mesh(mesh.devices.reshape(SIZES), AXES)
    placed = (
        P(LAYER, FEAT, None),
        P(LAYER, FEAT, None),
        P(LAYER, None, FEAT),
        P(LAYER, FEAT),
        P(LAYER, None, FEAT, None),
        P(LAYER, None),
    )
    return jax.shard_map(
        body,
        mesh=fine,
        in_specs=placed,
        out_specs=(
            P(LAYER, None, FEAT),
            P(LAYER, FEAT),
            P(LAYER, None, FEAT, None),
            P(LAYER, None),
            P(),
        ),
        check_vma=False,
    )
```

profile of v0, /device:TPU:1, one launch (start us, length us, event | category | flops | bytes accessed | tf_op | source)
XLA Modules:
  0.0 186.7 jit_solution(10501705085942699950)
XLA Ops:
  0.6 3.6 %collective-permute-start = (bf16[16,2304]{1,0:T(8,128)(2,1)}, bf16[16,2304]{1,0:T(8,128)(2,1)S(1)}, u32[]{:S(2)}, u32[]{:S(2)}) collective-permute-start(bf16[16,2304]{1,0:T(8,128)(2,1)} %bitcast.218), channel_id=1, source_target_pairs={{0,16},{16,0},{1,17},{17,1},{2,18},{18,2},{3,19},{19,3},{4,20},{20... | collective-permute-start | bytes 221192 | tf_op jit(solution)/shard_map/ppermute | solution.py:37
  8.7 2.6 %collective-permute-start.2 = (bf16[32,2304]{1,0:T(8,128)(2,1)S(1)}, bf16[32,2304]{1,0:T(8,128)(2,1)S(1)}, u32[]{:S(2)}, u32[]{:S(2)}) collective-permute-start(bf16[32,2304]{1,0:T(8,128)(2,1)S(1)} %pad_maximum_fusion.17), channel_id=1, source_target_pairs={{0,2},{1,3},{2,0},{3,1},{4,6},{5,7},{6,4},{7,5},{8,10},{9,11},{10,... | collective-permute-start | bytes 442376 | tf_op jit(solution)/shard_map/ppermute | solution.py:33
  13.1 2.6 %collective-permute-done.1 = bf16[32,2304]{1,0:T(8,128)(2,1)S(1)} collective-permute-done((bf16[32,2304]{1,0:T(8,128)(2,1)S(1)}, bf16[32,2304]{1,0:T(8,128)(2,1)S(1)}, u32[]{:S(2)}, u32[]{:S(2)}) %collective-permute-start.1) | collective-permute-done | bytes 147488 | tf_op jit(solution)/shard_map/ppermute | solution.py:33
  19.3 2.1 %collective-permute-start.4 = (bf16[128,2304]{1,0:T(8,128)(2,1)S(1)}, bf16[128,2304]{1,0:T(8,128)(2,1)S(1)}, u32[]{:S(2)}, u32[]{:S(2)}) collective-permute-start(bf16[128,2304]{1,0:T(8,128)(2,1)S(1)} %get-tuple-element.32), channel_id=1, source_target_pairs={{0,12},{1,13},{2,14},{3,15},{4,0},{5,1},{6,2},{7,3},{8,4},{9,5},{1... | collective-permute-start | bytes 1769480 | tf_op jit(solution)/shard_map/ppermute | solution.py:33
  23.4 3.9 %collective-permute-start.8 = (bf16[2,256,2304]{2,1,0:T(8,128)(2,1)S(1)}, bf16[2,256,2304]{2,1,0:T(8,128)(2,1)S(1)}, u32[]{:S(2)}, u32[]{:S(2)}) collective-permute-start(bf16[2,256,2304]{2,1,0:T(8,128)(2,1)S(1)} %dynamic-slice_bitcast_fusion), channel_id=1, source_target_pairs={{0,32},{32,0},{1,33},{33,1},{2,34},{34,2},{3,35},{35,3},{4,36},{36... | collective-permute-start | bytes 7077896 | tf_op jit(solution)/shard_map/ppermute | solution.py:37
  29.1 2.7 %collective-permute-start.5 = (bf16[64,2304]{1,0:T(8,128)(2,1)S(1)}, bf16[64,2304]{1,0:T(8,128)(2,1)S(1)}, u32[]{:S(2)}, u32[]{:S(2)}) collective-permute-start(bf16[64,2304]{1,0:T(8,128)(2,1)S(1)} %slice.163), channel_id=1, source_target_pairs={{0,12},{1,13},{2,14},{3,15},{4,0},{5,1},{6,2},{7,3},{8,4},{9,5},{1... | collective-permute-start | bytes 884744 | tf_op jit(solution)/shard_map/ppermute | solution.py:33
  32.7 2.8 %collective-permute-done.5 = bf16[64,2304]{1,0:T(8,128)(2,1)S(1)} collective-permute-done((bf16[64,2304]{1,0:T(8,128)(2,1)S(1)}, bf16[64,2304]{1,0:T(8,128)(2,1)S(1)}, u32[]{:S(2)}, u32[]{:S(2)}) %collective-permute-start.5) | collective-permute-done | bytes 294944 | tf_op jit(solution)/shard_map/ppermute | solution.py:33
  37.8 3.2 %maximum_convert_fusion = (bf16[512,256]{1,0:T(8,128)(2,1)S(1)}, f32[512,256]{1,0:T(8,128)}) fusion(f32[256]{0:T(256)S(1)} %bitcast.226, bf16[512,2304]{1,0:T(8,128)(2,1)} %constant_dynamic-update-slice_fusion.5, bf16[1,2304,256]{2,1,0:T(8,128)(2,1)S(1)} %copy-done), kind=kOutput, calls=%fused_computation.83 | convolution fusion | flops 604372992 | bytes 4326400 | tf_op jit(solution)/shard_map/dot_general | solution.py:92
  41.1 5.2 %collective-permute-start.9 = (bf16[512,256]{1,0:T(8,128)(2,1)S(1)}, bf16[512,256]{1,0:T(8,128)(2,1)S(1)}, u32[]{:S(2)}, u32[]{:S(2)}) collective-permute-start(bf16[512,256]{1,0:T(8,128)(2,1)S(1)} %get-tuple-element.42), channel_id=1, source_target_pairs={{0,32},{32,0},{1,33},{33,1},{2,34},{34,2},{3,35},{35,3},{4,36},{36... | collective-permute-start | bytes 786440 | tf_op jit(solution)/shard_map/ppermute | solution.py:37
  59.5 2.5 %fusion.8 = bf16[2,128,2304]{2,1,0:T(8,128)(2,1)S(1)} fusion(bf16[512,256]{1,0:T(8,128)(2,1)} %copy-done.5, bf16[512,256]{1,0:T(8,128)(2,1)} %bitcast.223, bf16[2,256,2304]{2,1,0:T(8,128)(2,1)} %copy-done.2, bf16[2,256,2304]{2,1,0:T(8,128)(2,1)S(1)} %bitcast_multiply_fusion), kind=kOutput, calls=%fused_computation.23 | convolution fusion | flops 614268928 | bytes 6422528 | tf_op jit(solution)/shard_map/tf,sfd->std/dot_general | solution.py:99
  62.0 8.1 %collective-permute-done.11 = bf16[2,128,2304]{2,1,0:T(8,128)(2,1)S(1)} collective-permute-done((bf16[2,128,2304]{2,1,0:T(8,128)(2,1)}, bf16[2,128,2304]{2,1,0:T(8,128)(2,1)S(1)}, u32[]{:S(2)}, u32[]{:S(2)}) %collective-permute-start.11) | collective-permute-done | bytes 1179680 | tf_op jit(solution)/shard_map/ppermute | solution.py:33
  70.1 12.0 %collective-permute-done.12 = bf16[2,128,2304]{2,1,0:T(8,128)(2,1)} collective-permute-done((bf16[2,128,2304]{2,1,0:T(8,128)(2,1)}, bf16[2,128,2304]{2,1,0:T(8,128)(2,1)}, u32[]{:S(2)}, u32[]{:S(2)}) %collective-permute-start.12) | collective-permute-done | bytes 1179680 | tf_op jit(solution)/shard_map/ppermute | solution.py:33
  83.2 2.6 %add_convert_fusion = bf16[2,128,2304]{2,1,0:T(8,128)(2,1)S(1)} fusion(bf16[2,128,2304]{2,1,0:T(8,128)(2,1)} %collective-permute-done.12, bf16[2,128,2304]{2,1,0:T(8,128)(2,1)} %copy-done.4, bf16[2,128,2304]{2,1,0:T(8,128)(2,1)} %collective-permute-done.10, bf16[2,128,2304]{2,1,0:T(8,128)(2,1)S(1)} %fusion.8), kind=kLoop, calls=%fused_computation.40 | loop fusion | flops 4718592 | bytes 5898240 | tf_op jit(solution)/shard_map/convert_element_type | solution.py:104
  94.2 4.2 %collective-permute-done.15 = bf16[2,32,2304]{2,1,0:T(8,128)(2,1)} collective-permute-done((bf16[2,32,2304]{2,1,0:T(8,128)(2,1)}, bf16[2,32,2304]{2,1,0:T(8,128)(2,1)}, u32[]{:S(2)}, u32[]{:S(2)}) %collective-permute-start.15) | collective-permute-done | bytes 294944 | tf_op jit(solution)/shard_map/ppermute | solution.py:33
  99.9 2.8 %collective-permute-start.16 = (bf16[2,2,16,2304]{3,2,1,0:T(8,128)(2,1)S(1)}, bf16[2,2,16,2304]{3,2,1,0:T(8,128)(2,1)S(1)}, u32[]{:S(2)}, u32[]{:S(2)}) collective-permute-start(bf16[2,2,16,2304]{3,2,1,0:T(8,128)(2,1)S(1)} %pad_maximum_fusion.15), channel_id=1, source_target_pairs={{0,16},{16,0},{1,17},{17,1},{2,18},{18,2},{3,19},{19,3},{4,20},{20... | collective-permute-start | bytes 884744 | tf_op jit(solution)/shard_map/ppermute | solution.py:37
  103.7 3.4 %collective-permute-done.16 = bf16[2,2,16,2304]{3,2,1,0:T(8,128)(2,1)S(1)} collective-permute-done((bf16[2,2,16,2304]{3,2,1,0:T(8,128)(2,1)S(1)}, bf16[2,2,16,2304]{3,2,1,0:T(8,128)(2,1)S(1)}, u32[]{:S(2)}, u32[]{:S(2)}) %collective-permute-start.16) | collective-permute-done | bytes 294944 | tf_op jit(solution)/shard_map/ppermute | solution.py:37
  107.2 4.4 %collective-permute-done.18 = bf16[2,16,2304]{2,1,0:T(8,128)(2,1)S(1)} collective-permute-done((bf16[2,16,2304]{2,1,0:T(8,128)(2,1)S(1)}, bf16[2,16,2304]{2,1,0:T(8,128)(2,1)S(1)}, u32[]{:S(2)}, u32[]{:S(2)}) %collective-permute-start.18) | collective-permute-done | bytes 147488 | tf_op jit(solution)/shard_map/ppermute | solution.py:113
  111.8 4.2 %collective-permute-start.20 = (bf16[2,32,2304]{2,1,0:T(8,128)(2,1)S(1)}, bf16[2,32,2304]{2,1,0:T(8,128)(2,1)S(1)}, u32[]{:S(2)}, u32[]{:S(2)}) collective-permute-start(bf16[2,32,2304]{2,1,0:T(8,128)(2,1)S(1)} %pad_maximum_fusion.16), channel_id=1, source_target_pairs={{0,2},{1,3},{2,0},{3,1},{4,6},{5,7},{6,4},{7,5},{8,10},{9,11},{10,... | collective-permute-start | bytes 884744 | tf_op jit(solution)/shard_map/ppermute | solution.py:33
  119.3 4.3 %collective-permute-done.20 = bf16[2,32,2304]{2,1,0:T(8,128)(2,1)S(1)} collective-permute-done((bf16[2,32,2304]{2,1,0:T(8,128)(2,1)S(1)}, bf16[2,32,2304]{2,1,0:T(8,128)(2,1)S(1)}, u32[]{:S(2)}, u32[]{:S(2)}) %collective-permute-start.20) | collective-permute-done | bytes 294944 | tf_op jit(solution)/shard_map/ppermute | solution.py:33
  123.8 3.0 %collective-permute-start.22 = (bf16[2,128,2304]{2,1,0:T(8,128)(2,1)S(1)}, bf16[2,128,2304]{2,1,0:T(8,128)(2,1)S(1)}, u32[]{:S(2)}, u32[]{:S(2)}) collective-permute-start(bf16[2,128,2304]{2,1,0:T(8,128)(2,1)S(1)} %bitcast.186), channel_id=1, source_target_pairs={{0,12},{1,13},{2,14},{3,15},{4,0},{5,1},{6,2},{7,3},{8,4},{9,5},{1... | collective-permute-start | bytes 3538952 | tf_op jit(solution)/shard_map/ppermute | solution.py:33
  126.8 2.4 %collective-permute-start.27 = (bf16[2,128,2304]{2,1,0:T(8,128)(2,1)S(1)}, bf16[2,128,2304]{2,1,0:T(8,128)(2,1)S(1)}, u32[]{:S(2)}, u32[]{:S(2)}) collective-permute-start(bf16[2,128,2304]{2,1,0:T(8,128)(2,1)S(1)} %bitcast.187), channel_id=1, source_target_pairs={{0,32},{32,0},{1,33},{33,1},{2,34},{34,2},{3,35},{35,3},{4,36},{36... | collective-permute-start | bytes 3538952 | tf_op jit(solution)/shard_map/ppermute | solution.py:37
  131.5 8.4 %collective-permute-done.22 = bf16[2,128,2304]{2,1,0:T(8,128)(2,1)S(1)} collective-permute-done((bf16[2,128,2304]{2,1,0:T(8,128)(2,1)S(1)}, bf16[2,128,2304]{2,1,0:T(8,128)(2,1)S(1)}, u32[]{:S(2)}, u32[]{:S(2)}) %collective-permute-start.22) | collective-permute-done | bytes 1179680 | tf_op jit(solution)/shard_map/ppermute | solution.py:33
  140.0 3.5 %collective-permute-start.23 = (bf16[1,128,2304]{2,1,0:T(8,128)(2,1)S(1)}, bf16[1,128,2304]{2,1,0:T(8,128)(2,1)S(1)}, u32[]{:S(2)}, u32[]{:S(2)}) collective-permute-start(bf16[1,128,2304]{2,1,0:T(8,128)(2,1)S(1)} %get-tuple-element.13), channel_id=1, source_target_pairs={{0,12},{1,13},{2,14},{3,15},{4,0},{5,1},{6,2},{7,3},{8,4},{9,5},{1... | collective-permute-start | bytes 1769480 | tf_op jit(solution)/shard_map/ppermute | solution.py:33
  143.5 2.3 %collective-permute-done.24 = bf16[2,128,2304]{2,1,0:T(8,128)(2,1)S(1)} collective-permute-done((bf16[2,128,2304]{2,1,0:T(8,128)(2,1)S(1)}, bf16[2,128,2304]{2,1,0:T(8,128)(2,1)S(1)}, u32[]{:S(2)}, u32[]{:S(2)}) %collective-permute-start.24) | collective-permute-done | bytes 1179680 | tf_op jit(solution)/shard_map/ppermute | solution.py:33
  152.3 3.9 %collective-permute-done.25 = bf16[1,128,2304]{2,1,0:T(8,128)(2,1)S(1)} collective-permute-done((bf16[1,128,2304]{2,1,0:T(8,128)(2,1)S(1)}, bf16[1,128,2304]{2,1,0:T(8,128)(2,1)S(1)}, u32[]{:S(2)}, u32[]{:S(2)}) %collective-permute-start.25) | collective-permute-done | bytes 589856 | tf_op jit(solution)/shard_map/ppermute | solution.py:33
  163.9 3.3 %collective-permute-start.32 = (f32[8,128]{1,0:T(8,128)S(1)}, f32[8,128]{1,0:T(8,128)S(1)}, u32[]{:S(2)}, u32[]{:S(2)}) collective-permute-start(f32[8,128]{1,0:T(8,128)S(1)} %broadcast_add_fusion), channel_id=1, source_target_pairs={{0,64},{1,65},{2,66},{3,67},{4,68},{5,69},{6,70},{7,71},{8,72},{9,... | collective-permute-start | bytes 12296 | tf_op jit(solution)/shard_map/ppermute | solution.py:161
  170.4 2.2 %convolution_bitcast_fusion = f32[1,2304,256]{2,1,0:T(8,128)} fusion(bf16[512,2304]{1,0:T(8,128)(2,1)S(1)} %copy-done.10, bf16[512,256]{1,0:T(8,128)(2,1)S(1)} %get-tuple-element.8), kind=kOutput, calls=%fused_computation.14 | convolution fusion | flops 603979776 | bytes 4980736 | tf_op jit(solution)/shard_map/dot_general | solution.py:132
  172.9 2.1 %fusion.5 = f32[1,256,2304]{2,1,0:T(8,128)S(1)} fusion(bf16[512,256]{1,0:T(8,128)(2,1)S(1)} %get-tuple-element.31, pred[]{:T(512)S(6)} %eq.31, pred[]{:T(512)S(6)} %le.13, bf16[128,2304]{1,0:T(8,128)(2,1)S(1)} %get-tuple-element.23, bf16[128,2304]{1,0:T(8,128)(2,1)S(1)} %get-tuple-element.21, bf16[128,2304]{1,0:T(8,128)(2,1)S(1)} %get-tuple-element.19, ...), kind=kOutput, calls=%fused_computation.16 | convolution fusion | flops 625213440 | bytes 7340034 | tf_op jit(solution)/shard_map/dot_general | solution.py:146
  175.0 2.1 %fusion.4 = f32[1,256,2304]{2,1,0:T(8,128)S(1)} fusion(bf16[512,256]{1,0:T(8,128)(2,1)S(1)} %get-tuple-element.30, pred[]{:T(512)S(6)} %eq.30, pred[]{:T(512)S(6)} %le.12, bf16[128,2304]{1,0:T(8,128)(2,1)S(1)} %get-tuple-element.23, bf16[128,2304]{1,0:T(8,128)(2,1)S(1)} %get-tuple-element.21, bf16[128,2304]{1,0:T(8,128)(2,1)S(1)} %get-tuple-element.19, ...), kind=kOutput, calls=%fused_computation.15 | convolution fusion | flops 625213440 | bytes 7340034 | tf_op jit(solution)/shard_map/dot_general | solution.py:146
  177.1 2.1 %fusion.6 = f32[1,256,2304]{2,1,0:T(8,128)S(1)} fusion(bf16[512,256]{1,0:T(8,128)(2,1)S(1)} %get-tuple-element.30, pred[]{:T(512)S(6)} %eq.30, pred[]{:T(512)S(6)} %le.14, bf16[128,2304]{1,0:T(8,128)(2,1)S(1)} %get-tuple-element.24, bf16[128,2304]{1,0:T(8,128)(2,1)S(1)} %get-tuple-element.22, bf16[128,2304]{1,0:T(8,128)(2,1)S(1)} %get-tuple-element.20, ...), kind=kOutput, calls=%fused_computation.17 | convolution fusion | flops 625213440 | bytes 7340034 | tf_op jit(solution)/shard_map/dot_general | solution.py:146
  179.2 2.1 %fusion.7 = f32[1,256,2304]{2,1,0:T(8,128)S(1)} fusion(bf16[512,256]{1,0:T(8,128)(2,1)S(1)} %get-tuple-element.31, pred[]{:T(512)S(6)} %eq.31, pred[]{:T(512)S(6)} %le.15, bf16[128,2304]{1,0:T(8,128)(2,1)S(1)} %get-tuple-element.24, bf16[128,2304]{1,0:T(8,128)(2,1)S(1)} %get-tuple-element.22, bf16[128,2304]{1,0:T(8,128)(2,1)S(1)} %get-tuple-element.20, ...), kind=kOutput, calls=%fused_computation.18 | convolution fusion | flops 625213440 | bytes 7340034 | tf_op jit(solution)/shard_map/dot_general | solution.py:146
  181.3 4.2 %maximum_bitcast_fusion = f32[1,4,256,2304]{3,2,1,0:T(8,128)} fusion(f32[1,256,2304]{2,1,0:T(8,128)S(1)} %fusion.7, f32[1,256,2304]{2,1,0:T(8,128)S(1)} %fusion.6, f32[1,256,2304]{2,1,0:T(8,128)S(1)} %fusion.5, f32[1,256,2304]{2,1,0:T(8,128)S(1)} %fusion.4), kind=kLoop, calls=%fused_computation | loop fusion | flops 7077888 | bytes 18874368 | tf_op jit(solution)/shard_map/broadcast_in_dim | solution.py:163
  (145 shorter events, 64.7 us)
Async XLA Ops:
  0.6 5.6 %collective-permute-start = (bf16[16,2304]{1,0:T(8,128)(2,1)}, bf16[16,2304]{1,0:T(8,128)(2,1)S(1)}, u32[]{:S(2)}, u32[]{:S(2)}) collective-permute-start(bf16[16,2304]{1,0:T(8,128)(2,1)} %bitcast.218), channel_id=1, source_target_pairs={{0,16},{16,0},{1,17},{17,1},{2,18},{18,2},{3,19},{19,3},{4,20},{20... | collective-permute-start | bytes 221192 | tf_op jit(solution)/shard_map/ppermute | solution.py:37
  7.1 9.9 %collective-permute-start.3 = (bf16[32,2304]{1,0:T(8,128)(2,1)S(1)}, bf16[32,2304]{1,0:T(8,128)(2,1)S(1)}, u32[]{:S(2)}, u32[]{:S(2)}) collective-permute-start(bf16[32,2304]{1,0:T(8,128)(2,1)S(1)} %pad_maximum_fusion.17), channel_id=1, source_target_pairs={{0,1},{1,2},{2,3},{3,0},{4,5},{5,6},{6,7},{7,4},{8,9},{9,10},{10,1... | collective-permute-start | bytes 442376 | tf_op jit(solution)/shard_map/ppermute | solution.py:33
  8.7 7.6 %collective-permute-start.2 = (bf16[32,2304]{1,0:T(8,128)(2,1)S(1)}, bf16[32,2304]{1,0:T(8,128)(2,1)S(1)}, u32[]{:S(2)}, u32[]{:S(2)}) collective-permute-start(bf16[32,2304]{1,0:T(8,128)(2,1)S(1)} %pad_maximum_fusion.17), channel_id=1, source_target_pairs={{0,2},{1,3},{2,0},{3,1},{4,6},{5,7},{6,4},{7,5},{8,10},{9,11},{10,... | collective-permute-start | bytes 442376 | tf_op jit(solution)/shard_map/ppermute | solution.py:33
  11.3 4.3 %collective-permute-start.1 = (bf16[32,2304]{1,0:T(8,128)(2,1)S(1)}, bf16[32,2304]{1,0:T(8,128)(2,1)S(1)}, u32[]{:S(2)}, u32[]{:S(2)}) collective-permute-start(bf16[32,2304]{1,0:T(8,128)(2,1)S(1)} %pad_maximum_fusion.17), channel_id=1, source_target_pairs={{0,3},{1,0},{2,1},{3,2},{4,7},{5,4},{6,5},{7,6},{8,11},{9,8},{10,9... | collective-permute-start | bytes 442376 | tf_op jit(solution)/shard_map/ppermute | solution.py:33
  17.7 11.3 %collective-permute-start.6 = (bf16[128,2304]{1,0:T(8,128)(2,1)S(1)}, bf16[128,2304]{1,0:T(8,128)(2,1)S(1)}, u32[]{:S(2)}, u32[]{:S(2)}) collective-permute-start(bf16[128,2304]{1,0:T(8,128)(2,1)S(1)} %get-tuple-element.32), channel_id=1, source_target_pairs={{0,4},{1,5},{2,6},{3,7},{4,8},{5,9},{6,10},{7,11},{8,12},{9,13},{1... | collective-permute-start | bytes 1769480 | tf_op jit(solution)/shard_map/ppermute | solution.py:33
  19.3 9.8 %collective-permute-start.4 = (bf16[128,2304]{1,0:T(8,128)(2,1)S(1)}, bf16[128,2304]{1,0:T(8,128)(2,1)S(1)}, u32[]{:S(2)}, u32[]{:S(2)}) collective-permute-start(bf16[128,2304]{1,0:T(8,128)(2,1)S(1)} %get-tuple-element.32), channel_id=1, source_target_pairs={{0,12},{1,13},{2,14},{3,15},{4,0},{5,1},{6,2},{7,3},{8,4},{9,5},{1... | collective-permute-start | bytes 1769480 | tf_op jit(solution)/shard_map/ppermute | solution.py:33
  23.4 24.1 %collective-permute-start.8 = (bf16[2,256,2304]{2,1,0:T(8,128)(2,1)S(1)}, bf16[2,256,2304]{2,1,0:T(8,128)(2,1)S(1)}, u32[]{:S(2)}, u32[]{:S(2)}) collective-permute-start(bf16[2,256,2304]{2,1,0:T(8,128)(2,1)S(1)} %dynamic-slice_bitcast_fusion), channel_id=1, source_target_pairs={{0,32},{32,0},{1,33},{33,1},{2,34},{34,2},{3,35},{35,3},{4,36},{36... | collective-permute-start | bytes 7077896 | tf_op jit(solution)/shard_map/ppermute | solution.py:37
  29.0 7.2 %collective-permute-start.7 = (bf16[64,2304]{1,0:T(8,128)(2,1)S(1)}, bf16[64,2304]{1,0:T(8,128)(2,1)S(1)}, u32[]{:S(2)}, u32[]{:S(2)}) collective-permute-start(bf16[64,2304]{1,0:T(8,128)(2,1)S(1)} %slice.164), channel_id=1, source_target_pairs={{0,4},{1,5},{2,6},{3,7},{4,8},{5,9},{6,10},{7,11},{8,12},{9,13},{1... | collective-permute-start | bytes 884744 | tf_op jit(solution)/shard_map/ppermute | solution.py:33
  29.1 6.4 %collective-permute-start.5 = (bf16[64,2304]{1,0:T(8,128)(2,1)S(1)}, bf16[64,2304]{1,0:T(8,128)(2,1)S(1)}, u32[]{:S(2)}, u32[]{:S(2)}) collective-permute-start(bf16[64,2304]{1,0:T(8,128)(2,1)S(1)} %slice.163), channel_id=1, source_target_pairs={{0,12},{1,13},{2,14},{3,15},{4,0},{5,1},{6,2},{7,3},{8,4},{9,5},{1... | collective-permute-start | bytes 884744 | tf_op jit(solution)/shard_map/ppermute | solution.py:33
  41.1 6.4 %collective-permute-start.9 = (bf16[512,256]{1,0:T(8,128)(2,1)S(1)}, bf16[512,256]{1,0:T(8,128)(2,1)S(1)}, u32[]{:S(2)}, u32[]{:S(2)}) collective-permute-start(bf16[512,256]{1,0:T(8,128)(2,1)S(1)} %get-tuple-element.42), channel_id=1, source_target_pairs={{0,32},{32,0},{1,33},{33,1},{2,34},{34,2},{3,35},{35,3},{4,36},{36... | collective-permute-start | bytes 786440 | tf_op jit(solution)/shard_map/ppermute | solution.py:37
  53.3 16.8 %collective-permute-start.11 = (bf16[2,128,2304]{2,1,0:T(8,128)(2,1)}, bf16[2,128,2304]{2,1,0:T(8,128)(2,1)S(1)}, u32[]{:S(2)}, u32[]{:S(2)}) collective-permute-start(bf16[2,128,2304]{2,1,0:T(8,128)(2,1)} %fusion.10), channel_id=1, source_target_pairs={{0,4},{1,5},{2,6},{3,7},{4,8},{5,9},{6,10},{7,11},{8,12},{9,13},{1... | collective-permute-start | bytes 3538952 | tf_op jit(solution)/shard_map/ppermute | solution.py:33
  54.1 28.0 %collective-permute-start.12 = (bf16[2,128,2304]{2,1,0:T(8,128)(2,1)}, bf16[2,128,2304]{2,1,0:T(8,128)(2,1)}, u32[]{:S(2)}, u32[]{:S(2)}) collective-permute-start(bf16[2,128,2304]{2,1,0:T(8,128)(2,1)} %fusion.11), channel_id=1, source_target_pairs={{0,12},{1,13},{2,14},{3,15},{4,0},{5,1},{6,2},{7,3},{8,4},{9,5},{1... | collective-permute-start | bytes 3538952 | tf_op jit(solution)/shard_map/ppermute | solution.py:33
  56.0 27.3 %collective-permute-start.10 = (bf16[2,128,2304]{2,1,0:T(8,128)(2,1)}, bf16[2,128,2304]{2,1,0:T(8,128)(2,1)}, u32[]{:S(2)}, u32[]{:S(2)}) collective-permute-start(bf16[2,128,2304]{2,1,0:T(8,128)(2,1)} %fusion.9), channel_id=1, source_target_pairs={{0,8},{1,9},{2,10},{3,11},{4,12},{5,13},{6,14},{7,15},{8,0},{9,1},... | collective-permute-start | bytes 3538952 | tf_op jit(solution)/shard_map/ppermute | solution.py:33
  86.8 7.4 %collective-permute-start.13 = (bf16[2,32,2304]{2,1,0:T(8,128)(2,1)}, bf16[2,32,2304]{2,1,0:T(8,128)(2,1)}, u32[]{:S(2)}, u32[]{:S(2)}) collective-permute-start(bf16[2,32,2304]{2,1,0:T(8,128)(2,1)} %get-tuple-element.27), channel_id=1, source_target_pairs={{0,2},{1,3},{2,0},{3,1},{4,6},{5,7},{6,4},{7,5},{8,10},{9,11},{10,... | collective-permute-start | bytes 884744 | tf_op jit(solution)/shard_map/ppermute | solution.py:33
  88.7 9.7 %collective-permute-start.15 = (bf16[2,32,2304]{2,1,0:T(8,128)(2,1)}, bf16[2,32,2304]{2,1,0:T(8,128)(2,1)}, u32[]{:S(2)}, u32[]{:S(2)}) collective-permute-start(bf16[2,32,2304]{2,1,0:T(8,128)(2,1)} %get-tuple-element.28), channel_id=1, source_target_pairs={{0,3},{1,0},{2,1},{3,2},{4,7},{5,4},{6,5},{7,6},{8,11},{9,8},{10,9... | collective-permute-start | bytes 884744 | tf_op jit(solution)/shard_map/ppermute | solution.py:33
  89.9 8.5 %collective-permute-start.14 = (bf16[2,32,2304]{2,1,0:T(8,128)(2,1)}, bf16[2,32,2304]{2,1,0:T(8,128)(2,1)}, u32[]{:S(2)}, u32[]{:S(2)}) collective-permute-start(bf16[2,32,2304]{2,1,0:T(8,128)(2,1)} %get-tuple-element.29), channel_id=1, source_target_pairs={{0,1},{1,2},{2,3},{3,0},{4,5},{5,6},{6,7},{7,4},{8,9},{9,10},{10,1... | collective-permute-start | bytes 884744 | tf_op jit(solution)/shard_map/ppermute | solution.py:33
  99.9 7.2 %collective-permute-start.16 = (bf16[2,2,16,2304]{3,2,1,0:T(8,128)(2,1)S(1)}, bf16[2,2,16,2304]{3,2,1,0:T(8,128)(2,1)S(1)}, u32[]{:S(2)}, u32[]{:S(2)}) collective-permute-start(bf16[2,2,16,2304]{3,2,1,0:T(8,128)(2,1)S(1)} %pad_maximum_fusion.15), channel_id=1, source_target_pairs={{0,16},{16,0},{1,17},{17,1},{2,18},{18,2},{3,19},{19,3},{4,20},{20... | collective-permute-start | bytes 884744 | tf_op jit(solution)/shard_map/ppermute | solution.py:37
  102.7 8.9 %collective-permute-start.18 = (bf16[2,16,2304]{2,1,0:T(8,128)(2,1)S(1)}, bf16[2,16,2304]{2,1,0:T(8,128)(2,1)S(1)}, u32[]{:S(2)}, u32[]{:S(2)}) collective-permute-start(bf16[2,16,2304]{2,1,0:T(8,128)(2,1)S(1)} %fusion.39), channel_id=1, source_target_pairs={{0,80},{16,64},{64,16},{80,0},{1,81},{17,65},{65,17},{81,1},{2,82}... | collective-permute-start | bytes 442376 | tf_op jit(solution)/shard_map/ppermute | solution.py:113
  103.7 7.9 %collective-permute-start.17 = (bf16[2,16,2304]{2,1,0:T(8,128)(2,1)S(1)}, bf16[2,16,2304]{2,1,0:T(8,128)(2,1)S(1)}, u32[]{:S(2)}, u32[]{:S(2)}) collective-permute-start(bf16[2,16,2304]{2,1,0:T(8,128)(2,1)S(1)} %fusion.39), channel_id=1, source_target_pairs={{0,64},{64,0},{1,65},{65,1},{2,66},{66,2},{3,67},{67,3},{4,68},{68... | collective-permute-start | bytes 442376 | tf_op jit(solution)/shard_map/ppermute | solution.py:37
  111.7 7.6 %collective-permute-start.21 = (bf16[2,32,2304]{2,1,0:T(8,128)(2,1)S(1)}, bf16[2,32,2304]{2,1,0:T(8,128)(2,1)S(1)}, u32[]{:S(2)}, u32[]{:S(2)}) collective-permute-start(bf16[2,32,2304]{2,1,0:T(8,128)(2,1)S(1)} %pad_maximum_fusion.16), channel_id=1, source_target_pairs={{0,1},{1,2},{2,3},{3,0},{4,5},{5,6},{6,7},{7,4},{8,9},{9,10},{10,1... | collective-permute-start | bytes 884744 | tf_op jit(solution)/shard_map/ppermute | solution.py:33
  111.8 11.8 %collective-permute-start.20 = (bf16[2,32,2304]{2,1,0:T(8,128)(2,1)S(1)}, bf16[2,32,2304]{2,1,0:T(8,128)(2,1)S(1)}, u32[]{:S(2)}, u32[]{:S(2)}) collective-permute-start(bf16[2,32,2304]{2,1,0:T(8,128)(2,1)S(1)} %pad_maximum_fusion.16), channel_id=1, source_target_pairs={{0,2},{1,3},{2,0},{3,1},{4,6},{5,7},{6,4},{7,5},{8,10},{9,11},{10,... | collective-permute-start | bytes 884744 | tf_op jit(solution)/shard_map/ppermute | solution.py:33
  116.0 7.6 %collective-permute-start.19 = (bf16[2,32,2304]{2,1,0:T(8,128)(2,1)S(1)}, bf16[2,32,2304]{2,1,0:T(8,128)(2,1)S(1)}, u32[]{:S(2)}, u32[]{:S(2)}) collective-permute-start(bf16[2,32,2304]{2,1,0:T(8,128)(2,1)S(1)} %pad_maximum_fusion.16), channel_id=1, source_target_pairs={{0,3},{1,0},{2,1},{3,2},{4,7},{5,4},{6,5},{7,6},{8,11},{9,8},{10,9... | collective-permute-start | bytes 884744 | tf_op jit(solution)/shard_map/ppermute | solution.py:33
  123.8 16.1 %collective-permute-start.22 = (bf16[2,128,2304]{2,1,0:T(8,128)(2,1)S(1)}, bf16[2,128,2304]{2,1,0:T(8,128)(2,1)S(1)}, u32[]{:S(2)}, u32[]{:S(2)}) collective-permute-start(bf16[2,128,2304]{2,1,0:T(8,128)(2,1)S(1)} %bitcast.186), channel_id=1, source_target_pairs={{0,12},{1,13},{2,14},{3,15},{4,0},{5,1},{6,2},{7,3},{8,4},{9,5},{1... | collective-permute-start | bytes 3538952 | tf_op jit(solution)/shard_map/ppermute | solution.py:33
  126.8 23.0 %collective-permute-start.27 = (bf16[2,128,2304]{2,1,0:T(8,128)(2,1)S(1)}, bf16[2,128,2304]{2,1,0:T(8,128)(2,1)S(1)}, u32[]{:S(2)}, u32[]{:S(2)}) collective-permute-start(bf16[2,128,2304]{2,1,0:T(8,128)(2,1)S(1)} %bitcast.187), channel_id=1, source_target_pairs={{0,32},{32,0},{1,33},{33,1},{2,34},{34,2},{3,35},{35,3},{4,36},{36... | collective-permute-start | bytes 3538952 | tf_op jit(solution)/shard_map/ppermute | solution.py:37
  129.2 16.6 %collective-permute-start.24 = (bf16[2,128,2304]{2,1,0:T(8,128)(2,1)S(1)}, bf16[2,128,2304]{2,1,0:T(8,128)(2,1)S(1)}, u32[]{:S(2)}, u32[]{:S(2)}) collective-permute-start(bf16[2,128,2304]{2,1,0:T(8,128)(2,1)S(1)} %bitcast.188), channel_id=1, source_target_pairs={{0,4},{1,5},{2,6},{3,7},{4,8},{5,9},{6,10},{7,11},{8,12},{9,13},{1... | collective-permute-start | bytes 3538952 | tf_op jit(solution)/shard_map/ppermute | solution.py:33
  140.0 12.2 %collective-permute-start.23 = (bf16[1,128,2304]{2,1,0:T(8,128)(2,1)S(1)}, bf16[1,128,2304]{2,1,0:T(8,128)(2,1)S(1)}, u32[]{:S(2)}, u32[]{:S(2)}) collective-permute-start(bf16[1,128,2304]{2,1,0:T(8,128)(2,1)S(1)} %get-tuple-element.13), channel_id=1, source_target_pairs={{0,12},{1,13},{2,14},{3,15},{4,0},{5,1},{6,2},{7,3},{8,4},{9,5},{1... | collective-permute-start | bytes 1769480 | tf_op jit(solution)/shard_map/ppermute | solution.py:33
  145.9 10.3 %collective-permute-start.25 = (bf16[1,128,2304]{2,1,0:T(8,128)(2,1)S(1)}, bf16[1,128,2304]{2,1,0:T(8,128)(2,1)S(1)}, u32[]{:S(2)}, u32[]{:S(2)}) collective-permute-start(bf16[1,128,2304]{2,1,0:T(8,128)(2,1)S(1)} %get-tuple-element.16), channel_id=1, source_target_pairs={{0,4},{1,5},{2,6},{3,7},{4,8},{5,9},{6,10},{7,11},{8,12},{9,13},{1... | collective-permute-start | bytes 1769480 | tf_op jit(solution)/shard_map/ppermute | solution.py:33
  146.0 26.7 %collective-permute-start.30 = (bf16[2,128,2304]{2,1,0:T(8,128)(2,1)S(1)}, bf16[2,128,2304]{2,1,0:T(8,128)(2,1)S(1)}, u32[]{:S(2)}, u32[]{:S(2)}) collective-permute-start(bf16[2,128,2304]{2,1,0:T(8,128)(2,1)S(1)} %collective-permute-done.24), channel_id=1, source_target_pairs={{0,32},{32,0},{1,33},{33,1},{2,34},{34,2},{3,35},{35,3},{4,36},{36... | collective-permute-start | bytes 3538952 | tf_op jit(solution)/shard_map/ppermute | solution.py:37
  147.0 25.7 %collective-permute-start.28 = (bf16[2,128,2304]{2,1,0:T(8,128)(2,1)S(1)}, bf16[2,128,2304]{2,1,0:T(8,128)(2,1)S(1)}, u32[]{:S(2)}, u32[]{:S(2)}) collective-permute-start(bf16[2,128,2304]{2,1,0:T(8,128)(2,1)S(1)} %collective-permute-done.22), channel_id=1, source_target_pairs={{0,32},{32,0},{1,33},{33,1},{2,34},{34,2},{3,35},{35,3},{4,36},{36... | collective-permute-start | bytes 3538952 | tf_op jit(solution)/shard_map/ppermute | solution.py:37
  157.0 15.9 %collective-permute-start.29 = (bf16[2,128,2304]{2,1,0:T(8,128)(2,1)S(1)}, bf16[2,128,2304]{2,1,0:T(8,128)(2,1)S(1)}, u32[]{:S(2)}, u32[]{:S(2)}) collective-permute-start(bf16[2,128,2304]{2,1,0:T(8,128)(2,1)S(1)} %constant_dynamic-update-slice_fusion.14), channel_id=1, source_target_pairs={{0,32},{32,0},{1,33},{33,1},{2,34},{34,2},{3,35},{35,3},{4,36},{36... | collective-permute-start | bytes 3538952 | tf_op jit(solution)/shard_map/ppermute | solution.py:37
  162.5 7.1 %collective-permute-start.26 = (f32[512,256]{1,0:T(8,128)S(1)}, f32[512,256]{1,0:T(8,128)S(1)}, u32[]{:S(2)}, u32[]{:S(2)}) collective-permute-start(f32[512,256]{1,0:T(8,128)S(1)} %slice.192), channel_id=1, source_target_pairs={{0,32},{32,0},{1,33},{33,1},{2,34},{34,2},{3,35},{35,3},{4,36},{36... | collective-permute-start | bytes 1572872 | tf_op jit(solution)/shard_map/ppermute | solution.py:37
  163.9 3.9 %collective-permute-start.32 = (f32[8,128]{1,0:T(8,128)S(1)}, f32[8,128]{1,0:T(8,128)S(1)}, u32[]{:S(2)}, u32[]{:S(2)}) collective-permute-start(f32[8,128]{1,0:T(8,128)S(1)} %broadcast_add_fusion), channel_id=1, source_target_pairs={{0,64},{1,65},{2,66},{3,67},{4,68},{5,69},{6,70},{7,71},{8,72},{9,... | collective-permute-start | bytes 12296 | tf_op jit(solution)/shard_map/ppermute | solution.py:161
  (15 other events, 176.2 us)
where the time goes:
time: 187 us
  waiting for transfers between devices  64.3 us (34%)
  starting transfers between devices  56.5 us (30%)
  matrix products  32.5 us (17%)
  other arithmetic  17 us (9%)
  local copies, waits for them, and re-layouts  13.5 us (7%)
  between operations  2.96 us (2%)
    ppermute x20, waiting for transfers between devices, move(): return lax.ppermute(value, PLANE, route(ring, step))  55.1 us
    ppermute x20, starting transfers between devices, move(): return lax.ppermute(value, PLANE, route(ring, step))  30.8 us
    ppermute x11, starting transfers between devices, swap(): return lax.ppermute(value, axis, [(0, 1), (1, 0)])  21.5 us
    dot_general x4, matrix products, body(): lax.dot_general(act, err, (((0,), (0,)), ((), ())), preferred_element_typ...  8.35 us
    dot_general x4, matrix products, body(): jnp.einsum('tf,sfd->std', blocks[k], weight, preferred_element_type=f32)  8.07 us
    dot_general x8, matrix products, back(): lax.dot_general(piece[slot], weight[slot], (((1,), (1,)), ((), ())), pref...  7.08 us
    unnamed x36, local copies, waits for them, and re-layouts  6 us
    ppermute x11, waiting for transfers between devices, swap(): return lax.ppermute(value, axis, [(0, 1), (1, 0)])  4.79 us
  transfers between devices with their start and end apart: 33, of which 17 were waited for; matrix products, arithmetic and copies ran while one was open for 20% of the time, Pallas kernels for 0%

commit v1 on v0

--- a/solution.py
+++ b/solution.py
@@ -46,8 +46,12 @@
     arrived = []
     for k in (2, 1, 3):
         arrived.append(move(blocks[k], ring, k))
-    total = blocks[0].astype(f32)
-    for piece in arrived:
+    return [blocks[0], *arrived]
+
+
+def summed(pieces):
+    total = pieces[0].astype(f32)
+    for piece in pieces[1:]:
         total = total + piece.astype(f32)
     return total
 
@@ -88,6 +92,7 @@
     own_valid = (slot + core >= layer).astype(bf16)[:, None, None]
     pair_valid = (slot + core >= layer + 1 - 2 * core).astype(bf16)[:, None, None]
     weight = jnp.concatenate([keep * own_valid, got * pair_valid], axis=1)
+    weight = lax.optimization_barrier(with_layout_constraint(weight, ROW_MAJOR))
 
     pre_act = jnp.dot(tokens_in, enc_weight[0], preferred_element_type=f32) + enc_bias[0]
     activity = jnp.maximum(pre_act, 0.0).astype(bf16)
@@ -99,10 +104,12 @@
         partial[k] = jnp.einsum(
             "tf,sfd->std", blocks[k], weight, preferred_element_type=f32
         ).astype(bf16)
+        partial[k] = with_layout_constraint(partial[k], ROW_MAJOR)
 
-    partial[0] = lax.optimization_barrier(with_layout_constraint(partial[0], ROW_MAJOR))
-    total = scatter4(partial, "u").astype(bf16).reshape(2, 4, 2 * rows, width)
-    total = scatter4([total[:, k] for k in range(4)], "v").reshape(2, 2, rows, width)
+    partial[0] = lax.optimization_barrier(partial[0])
+    pieces = [p.reshape(2, 4, 2 * rows, width) for p in scatter4(partial, "u")]
+    blocks = [summed([p[:, k] for p in pieces]).astype(bf16) for k in range(4)]
+    total = summed(scatter4(blocks, "v")).reshape(2, 2, rows, width)
 
     shift = dec_bias[0] - targets[0].astype(f32)
     owner = (jnp.arange(2) == x_lo).astype(f32)[:, None, None]
@@ -137,13 +144,16 @@
     )[None]
 
     errors = [[jnp.concatenate([p[k] for p in held]) for k in range(2)] for held in (mine, pair)]
-    orders = (activity, turned(activity))
+    products = [
+        [
+            lax.dot_general(act, err, (((0,), (0,)), ((), ())), preferred_element_type=f32)
+            for err in errs
+        ]
+        for act, errs in zip((activity, turned(activity)), errors)
+    ]
     slots = []
     for target in range(4):
-        parity = core == target % 2
-        err = jnp.where(parity, errors[0][target // 2], errors[1][target // 2])
-        act = jnp.where(parity, *orders)
-        grad = lax.dot_general(act, err, (((0,), (0,)), ((), ())), preferred_element_type=f32)
+        grad = jnp.where(core == target % 2, *[p[target // 2] for p in products])
         slots.append(jnp.where(target >= layer, grad / MB, 0.0))
     dec_grad = jnp.stack(slots)
 

time: 187 us -> 183 us (0.979)
  waiting for transfers between devices: 64.3 us -> 69.5 us
  other arithmetic: 17 us -> 13.3 us
  matrix products: 32.5 us -> 30.4 us
  local copies, waits for them, and re-layouts: 13.5 us -> 11.5 us
  starting transfers between devices: 56.5 us -> 54.6 us
    ppermute x20, waiting for transfers between devices: 55.1 us -> 60.2 us  [move(): return lax.ppermute(value, PLANE, route(ring, step))]
    dot_general x4, matrix products: 8.35 us -> 4.3 us  [body(): lax.dot_general(act, err, (((0,), (0,)), ((), ())), preferred_element_typ...]
    add x1 -> x3, other arithmetic: 1.28 us -> 4.04 us  [summed(): total = total + piece.astype(f32)]
    convert_element_type x1 -> x0, other arithmetic: 2.6 us -> none  [body(): total = scatter4(partial, 'u').astype(bf16).reshape(2, 4, 2 * rows, width)]
    unnamed x36 -> x30, local copies, waits for them, and re-layouts: 6 us -> 5.99 us
  transfers between devices with their start and end apart: 33 -> 33, of which waited for: 17 -> 18; matrix products, arithmetic and copies ran while one was open for 20% -> 20% of each run, Pallas kernels for 0% -> 0%
where the time goes in v1:
time: 183 us; the launch traced here: 182 us
  waiting for transfers between devices  69.5 us (38%)
  starting transfers between devices  54.6 us (30%)
  matrix products  30.4 us (17%)
  other arithmetic  13.3 us (7%)
  local copies, waits for them, and re-layouts  11.5 us (6%)
  between operations  2.95 us (2%)
    ppermute x20, waiting for transfers between devices, move(): return lax.ppermute(value, PLANE, route(ring, step))  60.2 us
    ppermute x20, starting transfers between devices, move(): return lax.ppermute(value, PLANE, route(ring, step))  30.6 us
    ppermute x11, starting transfers between devices, swap(): return lax.ppermute(value, axis, [(0, 1), (1, 0)])  20.1 us
    dot_general x4, matrix products, body(): jnp.einsum('tf,sfd->std', blocks[k], weight, preferred_element_type=f32)  9.16 us
    dot_general x8, matrix products, back(): lax.dot_general(piece[slot], weight[slot], (((1,), (1,)), ((), ())), pref...  8.75 us
    unnamed x30, local copies, waits for them, and re-layouts  5.99 us
    ppermute x11, waiting for transfers between devices, swap(): return lax.ppermute(value, axis, [(0, 1), (1, 0)])  4.78 us
    ppermute x1, waiting for transfers between devices, body(): other = lax.ppermute(terms[1], ('x_lo', 'x_hi'), ACROSS)  4.53 us
  transfers between devices with their start and end apart: 33, of which 18 were waited for; matrix products, arithmetic and copies ran while one was open for 20% of the time, Pallas kernels for 0%

profile of v1, /device:TPU:1, one launch (start us, length us, event | category | flops | bytes accessed | tf_op | source)
XLA Modules:
  0.0 182.3 jit_solution(10202886370928343134)
XLA Ops:
  0.6 3.6 %collective-permute-start = (bf16[16,2304]{1,0:T(8,128)(2,1)}, bf16[16,2304]{1,0:T(8,128)(2,1)S(1)}, u32[]{:S(2)}, u32[]{:S(2)}) collective-permute-start(bf16[16,2304]{1,0:T(8,128)(2,1)} %bitcast.279), channel_id=1, source_target_pairs={{0,16},{16,0},{1,17},{17,1},{2,18},{18,2},{3,19},{19,3},{4,20},{20... | collective-permute-start | bytes 221192 | tf_op jit(solution)/shard_map/ppermute | solution.py:37
  8.7 2.6 %collective-permute-start.2 = (bf16[32,2304]{1,0:T(8,128)(2,1)S(1)}, bf16[32,2304]{1,0:T(8,128)(2,1)S(1)}, u32[]{:S(2)}, u32[]{:S(2)}) collective-permute-start(bf16[32,2304]{1,0:T(8,128)(2,1)S(1)} %pad_maximum_fusion.5), channel_id=1, source_target_pairs={{0,2},{1,3},{2,0},{3,1},{4,6},{5,7},{6,4},{7,5},{8,10},{9,11},{10,... | collective-permute-start | bytes 442376 | tf_op jit(solution)/shard_map/ppermute | solution.py:33
  13.1 2.6 %collective-permute-done.1 = bf16[32,2304]{1,0:T(8,128)(2,1)S(1)} collective-permute-done((bf16[32,2304]{1,0:T(8,128)(2,1)S(1)}, bf16[32,2304]{1,0:T(8,128)(2,1)S(1)}, u32[]{:S(2)}, u32[]{:S(2)}) %collective-permute-start.1) | collective-permute-done | bytes 147488 | tf_op jit(solution)/shard_map/ppermute | solution.py:33
  19.3 2.1 %collective-permute-start.4 = (bf16[128,2304]{1,0:T(8,128)(2,1)S(1)}, bf16[128,2304]{1,0:T(8,128)(2,1)S(1)}, u32[]{:S(2)}, u32[]{:S(2)}) collective-permute-start(bf16[128,2304]{1,0:T(8,128)(2,1)S(1)} %get-tuple-element.31), channel_id=1, source_target_pairs={{0,12},{1,13},{2,14},{3,15},{4,0},{5,1},{6,2},{7,3},{8,4},{9,5},{1... | collective-permute-start | bytes 1769480 | tf_op jit(solution)/shard_map/ppermute | solution.py:33
  21.4 2.0 %dynamic-slice_bitcast_fusion = bf16[2,256,2304]{2,1,0:T(8,128)(2,1)S(1)} fusion(bf16[2,2,256,2304]{3,2,1,0:T(8,128)(2,1)} %bitcast.253, s32[]{:T(128)S(6)} %select_n.72), kind=kLoop, calls=%fused_computation.50 | loop fusion | bytes 4718596 | tf_op jit(solution)/shard_map/jit(dynamic_index_in_dim)/squeeze | solution.py:89
  23.4 3.9 %collective-permute-start.8 = (bf16[2,256,2304]{2,1,0:T(8,128)(2,1)S(1)}, bf16[2,256,2304]{2,1,0:T(8,128)(2,1)S(1)}, u32[]{:S(2)}, u32[]{:S(2)}) collective-permute-start(bf16[2,256,2304]{2,1,0:T(8,128)(2,1)S(1)} %dynamic-slice_bitcast_fusion), channel_id=1, source_target_pairs={{0,32},{32,0},{1,33},{33,1},{2,34},{34,2},{3,35},{35,3},{4,36},{36... | collective-permute-start | bytes 7077896 | tf_op jit(solution)/shard_map/ppermute | solution.py:37
  29.1 2.7 %collective-permute-start.5 = (bf16[64,2304]{1,0:T(8,128)(2,1)S(1)}, bf16[64,2304]{1,0:T(8,128)(2,1)S(1)}, u32[]{:S(2)}, u32[]{:S(2)}) collective-permute-start(bf16[64,2304]{1,0:T(8,128)(2,1)S(1)} %slice.211), channel_id=1, source_target_pairs={{0,12},{1,13},{2,14},{3,15},{4,0},{5,1},{6,2},{7,3},{8,4},{9,5},{1... | collective-permute-start | bytes 884744 | tf_op jit(solution)/shard_map/ppermute | solution.py:33
  32.7 2.8 %collective-permute-done.5 = bf16[64,2304]{1,0:T(8,128)(2,1)S(1)} collective-permute-done((bf16[64,2304]{1,0:T(8,128)(2,1)S(1)}, bf16[64,2304]{1,0:T(8,128)(2,1)S(1)}, u32[]{:S(2)}, u32[]{:S(2)}) %collective-permute-start.5) | collective-permute-done | bytes 294944 | tf_op jit(solution)/shard_map/ppermute | solution.py:33
  37.8 2.4 %maximum_convert_fusion = (bf16[512,256]{1,0:T(8,128)(2,1)S(1)}, f32[512,256]{1,0:T(8,128)S(1)}) fusion(f32[256]{0:T(256)S(1)} %bitcast.285, bf16[512,2304]{1,0:T(8,128)(2,1)} %constant_dynamic-update-slice_fusion.5, bf16[1,2304,256]{2,1,0:T(8,128)(2,1)S(1)} %copy-done), kind=kOutput, calls=%fused_computation.100 | convolution fusion | flops 604372992 | bytes 4326400 | tf_op jit(solution)/shard_map/dot_general | solution.py:97
  40.3 5.3 %collective-permute-start.9 = (bf16[512,256]{1,0:T(8,128)(2,1)S(1)}, bf16[512,256]{1,0:T(8,128)(2,1)S(1)}, u32[]{:S(2)}, u32[]{:S(2)}) collective-permute-start(bf16[512,256]{1,0:T(8,128)(2,1)S(1)} %get-tuple-element.41), channel_id=1, source_target_pairs={{0,32},{32,0},{1,33},{33,1},{2,34},{34,2},{3,35},{35,3},{4,36},{36... | collective-permute-start | bytes 786440 | tf_op jit(solution)/shard_map/ppermute | solution.py:37
  47.3 2.3 %fusion.1 = bf16[2,128,2304]{2,1,0:T(8,128)(2,1)} fusion(bf16[2,512,2304]{2,1,0:T(8,128)(2,1)S(1)} %pad_maximum_fusion, bf16[512,256]{1,0:T(8,128)(2,1)S(1)} %get-tuple-element.41, bf16[512,256]{1,0:T(8,128)(2,1)S(1)} %bitcast.249), kind=kOutput, calls=%fused_computation.8 | convolution fusion | flops 604831744 | bytes 6422528 | tf_op jit(solution)/shard_map/tf,sfd->std/dot_general | solution.py:104
  51.5 1.9 %fusion.2 = bf16[2,128,2304]{2,1,0:T(8,128)(2,1)} fusion(bf16[2,512,2304]{2,1,0:T(8,128)(2,1)S(1)} %pad_maximum_fusion, bf16[512,256]{1,0:T(8,128)(2,1)S(1)} %get-tuple-element.41, bf16[512,256]{1,0:T(8,128)(2,1)S(1)} %bitcast.251), kind=kOutput, calls=%fused_computation.9 | convolution fusion | flops 604831744 | bytes 6422528 | tf_op jit(solution)/shard_map/tf,sfd->std/dot_general | solution.py:104
  54.1 1.9 %collective-permute-start.12 = (bf16[2,128,2304]{2,1,0:T(8,128)(2,1)}, bf16[2,128,2304]{2,1,0:T(8,128)(2,1)}, u32[]{:S(2)}, u32[]{:S(2)}) collective-permute-start(bf16[2,128,2304]{2,1,0:T(8,128)(2,1)} %fusion.3), channel_id=1, source_target_pairs={{0,12},{1,13},{2,14},{3,15},{4,0},{5,1},{6,2},{7,3},{8,4},{9,5},{1... | collective-permute-start | bytes 3538952 | tf_op jit(solution)/shard_map/ppermute | solution.py:33
  56.6 3.2 %fusion = bf16[2,128,2304]{2,1,0:T(8,128)(2,1)S(1)} fusion(bf16[2,512,2304]{2,1,0:T(8,128)(2,1)} %copy-done.2, bf16[512,256]{1,0:T(8,128)(2,1)S(1)} %get-tuple-element.41, bf16[512,256]{1,0:T(8,128)(2,1)S(1)} %bitcast.252), kind=kOutput, calls=%fused_computation.7 | convolution fusion | flops 604831744 | bytes 6422528 | tf_op jit(solution)/shard_map/tf,sfd->std/dot_general | solution.py:104
  59.8 10.3 %collective-permute-done.11 = bf16[2,128,2304]{2,1,0:T(8,128)(2,1)S(1)} collective-permute-done((bf16[2,128,2304]{2,1,0:T(8,128)(2,1)}, bf16[2,128,2304]{2,1,0:T(8,128)(2,1)S(1)}, u32[]{:S(2)}, u32[]{:S(2)}) %collective-permute-start.11) | collective-permute-done | bytes 1179680 | tf_op jit(solution)/shard_map/ppermute | solution.py:33
  70.1 12.0 %collective-permute-done.12 = bf16[2,128,2304]{2,1,0:T(8,128)(2,1)} collective-permute-done((bf16[2,128,2304]{2,1,0:T(8,128)(2,1)}, bf16[2,128,2304]{2,1,0:T(8,128)(2,1)}, u32[]{:S(2)}, u32[]{:S(2)}) %collective-permute-start.12) | collective-permute-done | bytes 1179680 | tf_op jit(solution)/shard_map/ppermute | solution.py:33
  86.0 3.2 %collective-permute-start.15 = (bf16[2,32,2304]{2,1,0:T(8,128)(2,1)S(1)}, bf16[2,32,2304]{2,1,0:T(8,128)(2,1)S(1)}, u32[]{:S(2)}, u32[]{:S(2)}) collective-permute-start(bf16[2,32,2304]{2,1,0:T(8,128)(2,1)S(1)} %fusion.60), channel_id=1, source_target_pairs={{0,3},{1,0},{2,1},{3,2},{4,7},{5,4},{6,5},{7,6},{8,11},{9,8},{10,9... | collective-permute-start | bytes 884744 | tf_op jit(solution)/shard_map/ppermute | solution.py:33
  89.9 6.1 %collective-permute-done.15 = bf16[2,32,2304]{2,1,0:T(8,128)(2,1)S(1)} collective-permute-done((bf16[2,32,2304]{2,1,0:T(8,128)(2,1)S(1)}, bf16[2,32,2304]{2,1,0:T(8,128)(2,1)S(1)}, u32[]{:S(2)}, u32[]{:S(2)}) %collective-permute-start.15) | collective-permute-done | bytes 294944 | tf_op jit(solution)/shard_map/ppermute | solution.py:33
  96.6 2.8 %collective-permute-done.14 = bf16[2,32,2304]{2,1,0:T(8,128)(2,1)S(1)} collective-permute-done((bf16[2,32,2304]{2,1,0:T(8,128)(2,1)S(1)}, bf16[2,32,2304]{2,1,0:T(8,128)(2,1)S(1)}, u32[]{:S(2)}, u32[]{:S(2)}) %collective-permute-start.14) | collective-permute-done | bytes 294944 | tf_op jit(solution)/shard_map/ppermute | solution.py:33
  100.9 2.8 %collective-permute-start.16 = (bf16[2,2,16,2304]{3,2,1,0:T(8,128)(2,1)S(1)}, bf16[2,2,16,2304]{3,2,1,0:T(8,128)(2,1)S(1)}, u32[]{:S(2)}, u32[]{:S(2)}) collective-permute-start(bf16[2,2,16,2304]{3,2,1,0:T(8,128)(2,1)S(1)} %pad_maximum_fusion.3), channel_id=1, source_target_pairs={{0,16},{16,0},{1,17},{17,1},{2,18},{18,2},{3,19},{19,3},{4,20},{20... | collective-permute-start | bytes 884744 | tf_op jit(solution)/shard_map/ppermute | solution.py:37
  104.7 3.4 %collective-permute-done.16 = bf16[2,2,16,2304]{3,2,1,0:T(8,128)(2,1)S(1)} collective-permute-done((bf16[2,2,16,2304]{3,2,1,0:T(8,128)(2,1)S(1)}, bf16[2,2,16,2304]{3,2,1,0:T(8,128)(2,1)S(1)}, u32[]{:S(2)}, u32[]{:S(2)}) %collective-permute-start.16) | collective-permute-done | bytes 294944 | tf_op jit(solution)/shard_map/ppermute | solution.py:37
  108.3 4.5 %collective-permute-done.18 = bf16[2,16,2304]{2,1,0:T(8,128)(2,1)S(1)} collective-permute-done((bf16[2,16,2304]{2,1,0:T(8,128)(2,1)S(1)}, bf16[2,16,2304]{2,1,0:T(8,128)(2,1)S(1)}, u32[]{:S(2)}, u32[]{:S(2)}) %collective-permute-start.18) | collective-permute-done | bytes 147488 | tf_op jit(solution)/shard_map/ppermute | solution.py:120
  114.6 2.0 %collective-permute-start.19 = (bf16[2,32,2304]{2,1,0:T(8,128)(2,1)S(1)}, bf16[2,32,2304]{2,1,0:T(8,128)(2,1)S(1)}, u32[]{:S(2)}, u32[]{:S(2)}) collective-permute-start(bf16[2,32,2304]{2,1,0:T(8,128)(2,1)S(1)} %pad_maximum_fusion.4), channel_id=1, source_target_pairs={{0,3},{1,0},{2,1},{3,2},{4,7},{5,4},{6,5},{7,6},{8,11},{9,8},{10,9... | collective-permute-start | bytes 884744 | tf_op jit(solution)/shard_map/ppermute | solution.py:33
  116.6 6.3 %collective-permute-done.21 = bf16[2,32,2304]{2,1,0:T(8,128)(2,1)S(1)} collective-permute-done((bf16[2,32,2304]{2,1,0:T(8,128)(2,1)S(1)}, bf16[2,32,2304]{2,1,0:T(8,128)(2,1)S(1)}, u32[]{:S(2)}, u32[]{:S(2)}) %collective-permute-start.21) | collective-permute-done | bytes 294944 | tf_op jit(solution)/shard_map/ppermute | solution.py:33
  124.0 4.1 %collective-permute-start.22 = (bf16[2,128,2304]{2,1,0:T(8,128)(2,1)S(1)}, bf16[2,128,2304]{2,1,0:T(8,128)(2,1)S(1)}, u32[]{:S(2)}, u32[]{:S(2)}) collective-permute-start(bf16[2,128,2304]{2,1,0:T(8,128)(2,1)S(1)} %bitcast.243), channel_id=1, source_target_pairs={{0,12},{1,13},{2,14},{3,15},{4,0},{5,1},{6,2},{7,3},{8,4},{9,5},{1... | collective-permute-start | bytes 3538952 | tf_op jit(solution)/shard_map/ppermute | solution.py:33
  129.4 2.5 %fusion.43 = f32[128,512]{1,0:T(8,128)S(1)} fusion(bf16[128,2304]{1,0:T(8,128)(2,1)S(1)} %bitcast.271, bf16[2,512,2304]{2,1,0:T(8,128)(2,1)} %copy-done.2), kind=kOutput, calls=%fused_computation.58 | convolution fusion | flops 301989888 | bytes 3211264 | tf_op jit(solution)/shard_map/dot_general | solution.py:131
  133.1 8.1 %collective-permute-done.22 = bf16[2,128,2304]{2,1,0:T(8,128)(2,1)S(1)} collective-permute-done((bf16[2,128,2304]{2,1,0:T(8,128)(2,1)S(1)}, bf16[2,128,2304]{2,1,0:T(8,128)(2,1)S(1)}, u32[]{:S(2)}, u32[]{:S(2)}) %collective-permute-start.22) | collective-permute-done | bytes 1179680 | tf_op jit(solution)/shard_map/ppermute | solution.py:33
  141.4 3.5 %collective-permute-start.23 = (bf16[1,128,2304]{2,1,0:T(8,128)(2,1)S(1)}, bf16[1,128,2304]{2,1,0:T(8,128)(2,1)S(1)}, u32[]{:S(2)}, u32[]{:S(2)}) collective-permute-start(bf16[1,128,2304]{2,1,0:T(8,128)(2,1)S(1)} %get-tuple-element.25), channel_id=1, source_target_pairs={{0,12},{1,13},{2,14},{3,15},{4,0},{5,1},{6,2},{7,3},{8,4},{9,5},{1... | collective-permute-start | bytes 1769480 | tf_op jit(solution)/shard_map/ppermute | solution.py:33
  152.2 3.9 %collective-permute-done.25 = bf16[1,128,2304]{2,1,0:T(8,128)(2,1)S(1)} collective-permute-done((bf16[1,128,2304]{2,1,0:T(8,128)(2,1)S(1)}, bf16[1,128,2304]{2,1,0:T(8,128)(2,1)S(1)}, u32[]{:S(2)}, u32[]{:S(2)}) %collective-permute-start.25) | collective-permute-done | bytes 589856 | tf_op jit(solution)/shard_map/ppermute | solution.py:33
  165.1 3.0 %collective-permute-start.32 = (f32[8,128]{1,0:T(8,128)S(1)}, f32[8,128]{1,0:T(8,128)S(1)}, u32[]{:S(2)}, u32[]{:S(2)}) collective-permute-start(f32[8,128]{1,0:T(8,128)S(1)} %broadcast_add_fusion), channel_id=1, source_target_pairs={{0,64},{1,65},{2,66},{3,67},{4,68},{5,69},{6,70},{7,71},{8,72},{9,... | collective-permute-start | bytes 12296 | tf_op jit(solution)/shard_map/ppermute | solution.py:171
  171.7 2.2 %convolution_bitcast_fusion = f32[1,2304,256]{2,1,0:T(8,128)} fusion(bf16[512,2304]{1,0:T(8,128)(2,1)S(1)} %copy-done.5, bf16[512,256]{1,0:T(8,128)(2,1)S(1)} %get-tuple-element.8), kind=kOutput, calls=%fused_computation.2 | convolution fusion | flops 603979776 | bytes 4980736 | tf_op jit(solution)/shard_map/dot_general | solution.py:139
  176.9 4.2 %maximum_bitcast_fusion = f32[1,4,256,2304]{3,2,1,0:T(8,128)} fusion(f32[1,256,2304]{2,1,0:T(8,128)S(1)} %get-tuple-element.12, f32[1,256,2304]{2,1,0:T(8,128)S(1)} %get-tuple-element.11, f32[1,256,2304]{2,1,0:T(8,128)S(1)} %get-tuple-element.10, f32[1,256,2304]{2,1,0:T(8,128)S(1)} %get-tuple-element.9), kind=kLoop, calls=%fused_computation | loop fusion | flops 7077888 | bytes 18874368 | tf_op jit(solution)/shard_map/broadcast_in_dim | solution.py:173
  (139 shorter events, 54.9 us)
Async XLA Ops:
  0.6 5.6 %collective-permute-start = (bf16[16,2304]{1,0:T(8,128)(2,1)}, bf16[16,2304]{1,0:T(8,128)(2,1)S(1)}, u32[]{:S(2)}, u32[]{:S(2)}) collective-permute-start(bf16[16,2304]{1,0:T(8,128)(2,1)} %bitcast.279), channel_id=1, source_target_pairs={{0,16},{16,0},{1,17},{17,1},{2,18},{18,2},{3,19},{19,3},{4,20},{20... | collective-permute-start | bytes 221192 | tf_op jit(solution)/shard_map/ppermute | solution.py:37
  7.1 9.9 %collective-permute-start.3 = (bf16[32,2304]{1,0:T(8,128)(2,1)S(1)}, bf16[32,2304]{1,0:T(8,128)(2,1)S(1)}, u32[]{:S(2)}, u32[]{:S(2)}) collective-permute-start(bf16[32,2304]{1,0:T(8,128)(2,1)S(1)} %pad_maximum_fusion.5), channel_id=1, source_target_pairs={{0,1},{1,2},{2,3},{3,0},{4,5},{5,6},{6,7},{7,4},{8,9},{9,10},{10,1... | collective-permute-start | bytes 442376 | tf_op jit(solution)/shard_map/ppermute | solution.py:33
  8.7 7.6 %collective-permute-start.2 = (bf16[32,2304]{1,0:T(8,128)(2,1)S(1)}, bf16[32,2304]{1,0:T(8,128)(2,1)S(1)}, u32[]{:S(2)}, u32[]{:S(2)}) collective-permute-start(bf16[32,2304]{1,0:T(8,128)(2,1)S(1)} %pad_maximum_fusion.5), channel_id=1, source_target_pairs={{0,2},{1,3},{2,0},{3,1},{4,6},{5,7},{6,4},{7,5},{8,10},{9,11},{10,... | collective-permute-start | bytes 442376 | tf_op jit(solution)/shard_map/ppermute | solution.py:33
  11.3 4.3 %collective-permute-start.1 = (bf16[32,2304]{1,0:T(8,128)(2,1)S(1)}, bf16[32,2304]{1,0:T(8,128)(2,1)S(1)}, u32[]{:S(2)}, u32[]{:S(2)}) collective-permute-start(bf16[32,2304]{1,0:T(8,128)(2,1)S(1)} %pad_maximum_fusion.5), channel_id=1, source_target_pairs={{0,3},{1,0},{2,1},{3,2},{4,7},{5,4},{6,5},{7,6},{8,11},{9,8},{10,9... | collective-permute-start | bytes 442376 | tf_op jit(solution)/shard_map/ppermute | solution.py:33
  17.7 11.3 %collective-permute-start.6 = (bf16[128,2304]{1,0:T(8,128)(2,1)S(1)}, bf16[128,2304]{1,0:T(8,128)(2,1)S(1)}, u32[]{:S(2)}, u32[]{:S(2)}) collective-permute-start(bf16[128,2304]{1,0:T(8,128)(2,1)S(1)} %get-tuple-element.31), channel_id=1, source_target_pairs={{0,4},{1,5},{2,6},{3,7},{4,8},{5,9},{6,10},{7,11},{8,12},{9,13},{1... | collective-permute-start | bytes 1769480 | tf_op jit(solution)/shard_map/ppermute | solution.py:33
  19.3 9.8 %collective-permute-start.4 = (bf16[128,2304]{1,0:T(8,128)(2,1)S(1)}, bf16[128,2304]{1,0:T(8,128)(2,1)S(1)}, u32[]{:S(2)}, u32[]{:S(2)}) collective-permute-start(bf16[128,2304]{1,0:T(8,128)(2,1)S(1)} %get-tuple-element.31), channel_id=1, source_target_pairs={{0,12},{1,13},{2,14},{3,15},{4,0},{5,1},{6,2},{7,3},{8,4},{9,5},{1... | collective-permute-start | bytes 1769480 | tf_op jit(solution)/shard_map/ppermute | solution.py:33
  23.4 23.4 %collective-permute-start.8 = (bf16[2,256,2304]{2,1,0:T(8,128)(2,1)S(1)}, bf16[2,256,2304]{2,1,0:T(8,128)(2,1)S(1)}, u32[]{:S(2)}, u32[]{:S(2)}) collective-permute-start(bf16[2,256,2304]{2,1,0:T(8,128)(2,1)S(1)} %dynamic-slice_bitcast_fusion), channel_id=1, source_target_pairs={{0,32},{32,0},{1,33},{33,1},{2,34},{34,2},{3,35},{35,3},{4,36},{36... | collective-permute-start | bytes 7077896 | tf_op jit(solution)/shard_map/ppermute | solution.py:37
  29.0 7.2 %collective-permute-start.7 = (bf16[64,2304]{1,0:T(8,128)(2,1)S(1)}, bf16[64,2304]{1,0:T(8,128)(2,1)S(1)}, u32[]{:S(2)}, u32[]{:S(2)}) collective-permute-start(bf16[64,2304]{1,0:T(8,128)(2,1)S(1)} %slice.212), channel_id=1, source_target_pairs={{0,4},{1,5},{2,6},{3,7},{4,8},{5,9},{6,10},{7,11},{8,12},{9,13},{1... | collective-permute-start | bytes 884744 | tf_op jit(solution)/shard_map/ppermute | solution.py:33
  29.1 6.4 %collective-permute-start.5 = (bf16[64,2304]{1,0:T(8,128)(2,1)S(1)}, bf16[64,2304]{1,0:T(8,128)(2,1)S(1)}, u32[]{:S(2)}, u32[]{:S(2)}) collective-permute-start(bf16[64,2304]{1,0:T(8,128)(2,1)S(1)} %slice.211), channel_id=1, source_target_pairs={{0,12},{1,13},{2,14},{3,15},{4,0},{5,1},{6,2},{7,3},{8,4},{9,5},{1... | collective-permute-start | bytes 884744 | tf_op jit(solution)/shard_map/ppermute | solution.py:33
  40.3 6.4 %collective-permute-start.9 = (bf16[512,256]{1,0:T(8,128)(2,1)S(1)}, bf16[512,256]{1,0:T(8,128)(2,1)S(1)}, u32[]{:S(2)}, u32[]{:S(2)}) collective-permute-start(bf16[512,256]{1,0:T(8,128)(2,1)S(1)} %get-tuple-element.41), channel_id=1, source_target_pairs={{0,32},{32,0},{1,33},{33,1},{2,34},{34,2},{3,35},{35,3},{4,36},{36... | collective-permute-start | bytes 786440 | tf_op jit(solution)/shard_map/ppermute | solution.py:37
  53.3 16.8 %collective-permute-start.11 = (bf16[2,128,2304]{2,1,0:T(8,128)(2,1)}, bf16[2,128,2304]{2,1,0:T(8,128)(2,1)S(1)}, u32[]{:S(2)}, u32[]{:S(2)}) collective-permute-start(bf16[2,128,2304]{2,1,0:T(8,128)(2,1)} %fusion.2), channel_id=1, source_target_pairs={{0,4},{1,5},{2,6},{3,7},{4,8},{5,9},{6,10},{7,11},{8,12},{9,13},{1... | collective-permute-start | bytes 3538952 | tf_op jit(solution)/shard_map/ppermute | solution.py:33
  54.1 28.0 %collective-permute-start.12 = (bf16[2,128,2304]{2,1,0:T(8,128)(2,1)}, bf16[2,128,2304]{2,1,0:T(8,128)(2,1)}, u32[]{:S(2)}, u32[]{:S(2)}) collective-permute-start(bf16[2,128,2304]{2,1,0:T(8,128)(2,1)} %fusion.3), channel_id=1, source_target_pairs={{0,12},{1,13},{2,14},{3,15},{4,0},{5,1},{6,2},{7,3},{8,4},{9,5},{1... | collective-permute-start | bytes 3538952 | tf_op jit(solution)/shard_map/ppermute | solution.py:33
  56.0 27.3 %collective-permute-start.10 = (bf16[2,128,2304]{2,1,0:T(8,128)(2,1)}, bf16[2,128,2304]{2,1,0:T(8,128)(2,1)}, u32[]{:S(2)}, u32[]{:S(2)}) collective-permute-start(bf16[2,128,2304]{2,1,0:T(8,128)(2,1)} %fusion.1), channel_id=1, source_target_pairs={{0,8},{1,9},{2,10},{3,11},{4,12},{5,13},{6,14},{7,15},{8,0},{9,1},... | collective-permute-start | bytes 3538952 | tf_op jit(solution)/shard_map/ppermute | solution.py:33
  86.0 10.0 %collective-permute-start.15 = (bf16[2,32,2304]{2,1,0:T(8,128)(2,1)S(1)}, bf16[2,32,2304]{2,1,0:T(8,128)(2,1)S(1)}, u32[]{:S(2)}, u32[]{:S(2)}) collective-permute-start(bf16[2,32,2304]{2,1,0:T(8,128)(2,1)S(1)} %fusion.60), channel_id=1, source_target_pairs={{0,3},{1,0},{2,1},{3,2},{4,7},{5,4},{6,5},{7,6},{8,11},{9,8},{10,9... | collective-permute-start | bytes 884744 | tf_op jit(solution)/shard_map/ppermute | solution.py:33
  89.2 7.4 %collective-permute-start.13 = (bf16[2,32,2304]{2,1,0:T(8,128)(2,1)S(1)}, bf16[2,32,2304]{2,1,0:T(8,128)(2,1)S(1)}, u32[]{:S(2)}, u32[]{:S(2)}) collective-permute-start(bf16[2,32,2304]{2,1,0:T(8,128)(2,1)S(1)} %get-tuple-element.13), channel_id=1, source_target_pairs={{0,2},{1,3},{2,0},{3,1},{4,6},{5,7},{6,4},{7,5},{8,10},{9,11},{10,... | collective-permute-start | bytes 884744 | tf_op jit(solution)/shard_map/ppermute | solution.py:33
  89.2 10.2 %collective-permute-start.14 = (bf16[2,32,2304]{2,1,0:T(8,128)(2,1)S(1)}, bf16[2,32,2304]{2,1,0:T(8,128)(2,1)S(1)}, u32[]{:S(2)}, u32[]{:S(2)}) collective-permute-start(bf16[2,32,2304]{2,1,0:T(8,128)(2,1)S(1)} %get-tuple-element.14), channel_id=1, source_target_pairs={{0,1},{1,2},{2,3},{3,0},{4,5},{5,6},{6,7},{7,4},{8,9},{9,10},{10,1... | collective-permute-start | bytes 884744 | tf_op jit(solution)/shard_map/ppermute | solution.py:33
  100.9 7.2 %collective-permute-start.16 = (bf16[2,2,16,2304]{3,2,1,0:T(8,128)(2,1)S(1)}, bf16[2,2,16,2304]{3,2,1,0:T(8,128)(2,1)S(1)}, u32[]{:S(2)}, u32[]{:S(2)}) collective-permute-start(bf16[2,2,16,2304]{3,2,1,0:T(8,128)(2,1)S(1)} %pad_maximum_fusion.3), channel_id=1, source_target_pairs={{0,16},{16,0},{1,17},{17,1},{2,18},{18,2},{3,19},{19,3},{4,20},{20... | collective-permute-start | bytes 884744 | tf_op jit(solution)/shard_map/ppermute | solution.py:37
  103.8 9.0 %collective-permute-start.18 = (bf16[2,16,2304]{2,1,0:T(8,128)(2,1)S(1)}, bf16[2,16,2304]{2,1,0:T(8,128)(2,1)S(1)}, u32[]{:S(2)}, u32[]{:S(2)}) collective-permute-start(bf16[2,16,2304]{2,1,0:T(8,128)(2,1)S(1)} %fusion.67), channel_id=1, source_target_pairs={{0,80},{16,64},{64,16},{80,0},{1,81},{17,65},{65,17},{81,1},{2,82}... | collective-permute-start | bytes 442376 | tf_op jit(solution)/shard_map/ppermute | solution.py:120
  104.7 8.1 %collective-permute-start.17 = (bf16[2,16,2304]{2,1,0:T(8,128)(2,1)S(1)}, bf16[2,16,2304]{2,1,0:T(8,128)(2,1)S(1)}, u32[]{:S(2)}, u32[]{:S(2)}) collective-permute-start(bf16[2,16,2304]{2,1,0:T(8,128)(2,1)S(1)} %fusion.67), channel_id=1, source_target_pairs={{0,64},{64,0},{1,65},{65,1},{2,66},{66,2},{3,67},{67,3},{4,68},{68... | collective-permute-start | bytes 442376 | tf_op jit(solution)/shard_map/ppermute | solution.py:37
  112.9 10.1 %collective-permute-start.21 = (bf16[2,32,2304]{2,1,0:T(8,128)(2,1)S(1)}, bf16[2,32,2304]{2,1,0:T(8,128)(2,1)S(1)}, u32[]{:S(2)}, u32[]{:S(2)}) collective-permute-start(bf16[2,32,2304]{2,1,0:T(8,128)(2,1)S(1)} %pad_maximum_fusion.4), channel_id=1, source_target_pairs={{0,1},{1,2},{2,3},{3,0},{4,5},{5,6},{6,7},{7,4},{8,9},{9,10},{10,1... | collective-permute-start | bytes 884744 | tf_op jit(solution)/shard_map/ppermute | solution.py:33
  113.0 10.0 %collective-permute-start.20 = (bf16[2,32,2304]{2,1,0:T(8,128)(2,1)S(1)}, bf16[2,32,2304]{2,1,0:T(8,128)(2,1)S(1)}, u32[]{:S(2)}, u32[]{:S(2)}) collective-permute-start(bf16[2,32,2304]{2,1,0:T(8,128)(2,1)S(1)} %pad_maximum_fusion.4), channel_id=1, source_target_pairs={{0,2},{1,3},{2,0},{3,1},{4,6},{5,7},{6,4},{7,5},{8,10},{9,11},{10,... | collective-permute-start | bytes 884744 | tf_op jit(solution)/shard_map/ppermute | solution.py:33
  114.6 9.2 %collective-permute-start.19 = (bf16[2,32,2304]{2,1,0:T(8,128)(2,1)S(1)}, bf16[2,32,2304]{2,1,0:T(8,128)(2,1)S(1)}, u32[]{:S(2)}, u32[]{:S(2)}) collective-permute-start(bf16[2,32,2304]{2,1,0:T(8,128)(2,1)S(1)} %pad_maximum_fusion.4), channel_id=1, source_target_pairs={{0,3},{1,0},{2,1},{3,2},{4,7},{5,4},{6,5},{7,6},{8,11},{9,8},{10,9... | collective-permute-start | bytes 884744 | tf_op jit(solution)/shard_map/ppermute | solution.py:33
  124.0 17.3 %collective-permute-start.22 = (bf16[2,128,2304]{2,1,0:T(8,128)(2,1)S(1)}, bf16[2,128,2304]{2,1,0:T(8,128)(2,1)S(1)}, u32[]{:S(2)}, u32[]{:S(2)}) collective-permute-start(bf16[2,128,2304]{2,1,0:T(8,128)(2,1)S(1)} %bitcast.243), channel_id=1, source_target_pairs={{0,12},{1,13},{2,14},{3,15},{4,0},{5,1},{6,2},{7,3},{8,4},{9,5},{1... | collective-permute-start | bytes 3538952 | tf_op jit(solution)/shard_map/ppermute | solution.py:33
  128.2 21.5 %collective-permute-start.27 = (bf16[2,128,2304]{2,1,0:T(8,128)(2,1)S(1)}, bf16[2,128,2304]{2,1,0:T(8,128)(2,1)S(1)}, u32[]{:S(2)}, u32[]{:S(2)}) collective-permute-start(bf16[2,128,2304]{2,1,0:T(8,128)(2,1)S(1)} %bitcast.244), channel_id=1, source_target_pairs={{0,32},{32,0},{1,33},{33,1},{2,34},{34,2},{3,35},{35,3},{4,36},{36... | collective-permute-start | bytes 3538952 | tf_op jit(solution)/shard_map/ppermute | solution.py:37
  129.1 16.6 %collective-permute-start.24 = (bf16[2,128,2304]{2,1,0:T(8,128)(2,1)S(1)}, bf16[2,128,2304]{2,1,0:T(8,128)(2,1)S(1)}, u32[]{:S(2)}, u32[]{:S(2)}) collective-permute-start(bf16[2,128,2304]{2,1,0:T(8,128)(2,1)S(1)} %bitcast.245), channel_id=1, source_target_pairs={{0,4},{1,5},{2,6},{3,7},{4,8},{5,9},{6,10},{7,11},{8,12},{9,13},{1... | collective-permute-start | bytes 3538952 | tf_op jit(solution)/shard_map/ppermute | solution.py:33
  141.4 10.8 %collective-permute-start.23 = (bf16[1,128,2304]{2,1,0:T(8,128)(2,1)S(1)}, bf16[1,128,2304]{2,1,0:T(8,128)(2,1)S(1)}, u32[]{:S(2)}, u32[]{:S(2)}) collective-permute-start(bf16[1,128,2304]{2,1,0:T(8,128)(2,1)S(1)} %get-tuple-element.25), channel_id=1, source_target_pairs={{0,12},{1,13},{2,14},{3,15},{4,0},{5,1},{6,2},{7,3},{8,4},{9,5},{1... | collective-permute-start | bytes 1769480 | tf_op jit(solution)/shard_map/ppermute | solution.py:33
  145.8 10.3 %collective-permute-start.25 = (bf16[1,128,2304]{2,1,0:T(8,128)(2,1)S(1)}, bf16[1,128,2304]{2,1,0:T(8,128)(2,1)S(1)}, u32[]{:S(2)}, u32[]{:S(2)}) collective-permute-start(bf16[1,128,2304]{2,1,0:T(8,128)(2,1)S(1)} %get-tuple-element.28), channel_id=1, source_target_pairs={{0,4},{1,5},{2,6},{3,7},{4,8},{5,9},{6,10},{7,11},{8,12},{9,13},{1... | collective-permute-start | bytes 1769480 | tf_op jit(solution)/shard_map/ppermute | solution.py:33
  145.9 28.0 %collective-permute-start.30 = (bf16[2,128,2304]{2,1,0:T(8,128)(2,1)S(1)}, bf16[2,128,2304]{2,1,0:T(8,128)(2,1)S(1)}, u32[]{:S(2)}, u32[]{:S(2)}) collective-permute-start(bf16[2,128,2304]{2,1,0:T(8,128)(2,1)S(1)} %collective-permute-done.24), channel_id=1, source_target_pairs={{0,32},{32,0},{1,33},{33,1},{2,34},{34,2},{3,35},{35,3},{4,36},{36... | collective-permute-start | bytes 3538952 | tf_op jit(solution)/shard_map/ppermute | solution.py:37
  146.9 27.1 %collective-permute-start.28 = (bf16[2,128,2304]{2,1,0:T(8,128)(2,1)S(1)}, bf16[2,128,2304]{2,1,0:T(8,128)(2,1)S(1)}, u32[]{:S(2)}, u32[]{:S(2)}) collective-permute-start(bf16[2,128,2304]{2,1,0:T(8,128)(2,1)S(1)} %collective-permute-done.22), channel_id=1, source_target_pairs={{0,32},{32,0},{1,33},{33,1},{2,34},{34,2},{3,35},{35,3},{4,36},{36... | collective-permute-start | bytes 3538952 | tf_op jit(solution)/shard_map/ppermute | solution.py:37
  156.9 17.2 %collective-permute-start.29 = (bf16[2,128,2304]{2,1,0:T(8,128)(2,1)S(1)}, bf16[2,128,2304]{2,1,0:T(8,128)(2,1)S(1)}, u32[]{:S(2)}, u32[]{:S(2)}) collective-permute-start(bf16[2,128,2304]{2,1,0:T(8,128)(2,1)S(1)} %constant_dynamic-update-slice_fusion.14), channel_id=1, source_target_pairs={{0,32},{32,0},{1,33},{33,1},{2,34},{34,2},{3,35},{35,3},{4,36},{36... | collective-permute-start | bytes 3538952 | tf_op jit(solution)/shard_map/ppermute | solution.py:37
  160.4 4.0 %collective-permute-start.31 = (f32[8,128]{1,0:T(8,128)S(1)}, f32[8,128]{1,0:T(8,128)S(1)}, u32[]{:S(2)}, u32[]{:S(2)}) collective-permute-start(f32[8,128]{1,0:T(8,128)S(1)} %broadcast_in_dim.47), channel_id=1, source_target_pairs={{0,32},{32,0},{1,33},{33,1},{2,34},{34,2},{3,35},{35,3},{4,36},{36... | collective-permute-start | bytes 12296 | tf_op jit(solution)/shard_map/ppermute | solution.py:37
  163.1 7.8 %collective-permute-start.26 = (f32[512,256]{1,0:T(8,128)S(1)}, f32[512,256]{1,0:T(8,128)S(1)}, u32[]{:S(2)}, u32[]{:S(2)}) collective-permute-start(f32[512,256]{1,0:T(8,128)S(1)} %slice.250), channel_id=1, source_target_pairs={{0,32},{32,0},{1,33},{33,1},{2,34},{34,2},{3,35},{35,3},{4,36},{36... | collective-permute-start | bytes 1572872 | tf_op jit(solution)/shard_map/ppermute | solution.py:37
  (12 other events, 179.6 us)
